TPU v7x, 256 devices: a whole 4x4x8 slice. The times are simulated.
256 devices in a mesh: tp: 32 (over z, y), dp: 8 (over x, core).
Axes of the slice: x: 4, y: 4, z: 8, core: 2. Of those that a mesh axis runs over, the one named last changes fastest.
Arguments:
- x_in: bfloat16 [16384, 896], P('dp')
- w_gate: bfloat16 [896, 4864], P('dp', 'tp')
- w_up: bfloat16 [896, 4864], P('dp', 'tp')
- w_down: bfloat16 [4864, 896], P('tp', 'dp')
- dy_in: bfloat16 [16384, 896], P('dp')
Outputs:
- output 1: bfloat16 [16384, 896], P('dp')
- output 2: bfloat16 [16384, 896], P('dp')
- output 3: float32 [896, 4864], P('dp', 'tp')
- output 4: float32 [896, 4864], P('dp', 'tp')
- output 5: float32 [4864, 896], P('tp', 'dp')
All inputs are finite; a program needn't handle non-finite values.
Results may differ from a plain program's by a relative error of at most 0.001.
Values are sent between devices in bfloat16 or wider.
A program may use at most 768 MiB of HBM per device.

v0:
```python
import jax
import jax.numpy as jnp
from jax import lax
from jax.sharding import PartitionSpec as P


def solution(mesh):
    def device_pass(x_rows, gate_blk, up_blk, down_blk, dy_rows):
        x_cols = lax.all_to_all(x_rows, 'dp', 1, 0, tiled=True)
        gate_part = jnp.dot(x_cols, gate_blk, preferred_element_type=jnp.float32)
        up_part = jnp.dot(x_cols, up_blk, preferred_element_type=jnp.float32)
        gate_pre = lax.psum_scatter(gate_part, 'dp', scatter_dimension=0, tiled=True)
        up_pre = lax.psum_scatter(up_part, 'dp', scatter_dimension=0, tiled=True)
        sig_gate = jax.nn.sigmoid(gate_pre)
        silu_gate = gate_pre * sig_gate
        hidden = (silu_gate * up_pre).astype(jnp.bfloat16)
        hidden_all = lax.all_gather(hidden, 'dp', axis=0, tiled=True)
        out_part = jnp.dot(hidden_all, down_blk, preferred_element_type=jnp.float32)
        y_cols = (x_cols.astype(jnp.float32) + lax.psum(out_part, 'tp')).astype(jnp.bfloat16)
        y_rows = lax.all_to_all(y_cols, 'dp', 0, 1, tiled=True)
        dy_cols = lax.all_to_all(dy_rows, 'dp', 1, 0, tiled=True)
        grad_part = jnp.einsum('td,fd->tf', dy_cols, down_blk, preferred_element_type=jnp.float32)
        grad_h = lax.psum_scatter(grad_part, 'dp', scatter_dimension=0, tiled=True)
        d_gate = (grad_h * up_pre * sig_gate * (1.0 + gate_pre * (1.0 - sig_gate))).astype(jnp.bfloat16)
        d_up = (grad_h * silu_gate).astype(jnp.bfloat16)
        gate_all = lax.all_gather(d_gate, 'dp', axis=0, tiled=True)
        up_all = lax.all_gather(d_up, 'dp', axis=0, tiled=True)
        dx_part = (jnp.einsum('tf,df->td', gate_all, gate_blk, preferred_element_type=jnp.float32)
                   + jnp.einsum('tf,df->td', up_all, up_blk, preferred_element_type=jnp.float32))
        dx_cols = (dy_cols.astype(jnp.float32) + lax.psum(dx_part, 'tp')).astype(jnp.bfloat16)
        dx_rows = lax.all_to_all(dx_cols, 'dp', 0, 1, tiled=True)
        dw_gate = jnp.einsum('td,tf->df', x_cols, gate_all, preferred_element_type=jnp.float32)
        dw_up = jnp.einsum('td,tf->df', x_cols, up_all, preferred_element_type=jnp.float32)
        dw_down = jnp.einsum('tf,td->fd', hidden_all, dy_cols, preferred_element_type=jnp.float32)
        return y_rows, dx_rows, dw_gate, dw_up, dw_down

    row_spec = P('dp', None)
    weight_spec = P('dp', 'tp')
    down_spec = P('tp', 'dp')
    return jax.shard_map(device_pass, mesh=mesh,
                         in_specs=(row_spec, weight_spec, weight_spec, down_spec, row_spec),
                         out_specs=(row_spec, row_spec, weight_spec, weight_spec, down_spec),
                         check_vma=False)
```

profile of v0, /device:TPU:1, one launch (start us, length us, event | category | flops | bytes accessed | tf_op | source)
XLA Modules:
  0.0 847.1 jit_solution(4643765430918901152)
XLA Ops:
  7.2 6.1 copy.17
  13.3 49.6 %all_to_all.76 = bf16[2048,8,112]{0,2,1:T(8,128)(2,1)S(1)} all-to-all(bf16[2048,8,112]{0,2,1:T(8,128)(2,1)} %bitcast.60), channel_id=1, replica_groups=mesh['tp'=32,'dp'=8] {'dp'}, dimensions={1} | all-to-all | bytes 7340032 | tf_op jit(solution)/shard_map/all_to_all | solution.py:21
  63.3 1.8 copy-done.4
  65.2 5.3 fusion.4
  70.5 6.1 copy.14
  76.6 66.8 %all_to_all.77 = bf16[2048,8,112]{0,2,1:T(8,128)(2,1)S(1)} all-to-all(bf16[2048,8,112]{0,2,1:T(8,128)(2,1)} %bitcast.61), channel_id=1, replica_groups=mesh['tp'=32,'dp'=8] {'dp'}, dimensions={1} | all-to-all | bytes 7340032 | tf_op jit(solution)/shard_map/all_to_all | solution.py:9
  143.8 1.8 copy-done.2
  145.7 5.2 fusion.2
  151.0 7.3 fusion.1
  158.3 13.1 %reduce-scatter.8.cloned.1.call-done = f32[2048,152]{0,1:T(8,128)} async-done(((f32[16384,152]{0,1:T(8,128)}), f32[2048,152]{0,1:T(8,128)}) %reduce-scatter.8.cloned.1.call-update) | async-done | bytes 1245200 | tf_op jit(solution)/shard_map/reduce_scatter | solution.py:23
  171.4 65.5 %reduce-scatter.6.cloned.1.call-done = f32[2048,152]{0,1:T(8,128)} async-done(((f32[16384,152]{0,1:T(8,128)}), f32[2048,152]{0,1:T(8,128)}) %reduce-scatter.6.cloned.1.call-update) | async-done | bytes 1245200 | tf_op jit(solution)/shard_map/reduce_scatter | solution.py:13
  236.9 64.8 %reduce-scatter.4.cloned.1.call-done = f32[2048,152]{0,1:T(8,128)} async-done(((f32[16384,152]{0,1:T(8,128)}), f32[2048,152]{0,1:T(8,128)}) %reduce-scatter.4.cloned.1.call-update) | async-done | bytes 1245200 | tf_op jit(solution)/shard_map/reduce_scatter | solution.py:12
  301.8 4.1 multiply_convert_fusion
  307.2 37.1 %all-gather.6.cloned.1.call-done = bf16[16384,152]{0,1:T(8,128)(2,1)} async-done(((bf16[2048,152]{0,1:T(8,128)(2,1)}), bf16[16384,152]{0,1:T(8,128)(2,1)}) %all-gather.6.cloned.1.call-update) | async-done | bytes 4980752 | tf_op jit(solution)/shard_map/all_gather | solution.py:26
  344.2 6.5 fusion.5
  350.7 32.9 %all-gather.4.cloned.1.call-done = bf16[16384,152]{0,1:T(8,128)(2,1)} async-done(((bf16[2048,152]{0,1:T(8,128)(2,1)}), bf16[16384,152]{0,1:T(8,128)(2,1)}) %all-gather.4.cloned.1.call-update) | async-done | bytes 4980752 | tf_op jit(solution)/shard_map/all_gather | solution.py:17
  383.6 6.5 fusion.3
  390.1 32.9 %all-gather.8.cloned.1.call-done = bf16[16384,152]{0,1:T(8,128)(2,1)} async-done(((bf16[2048,152]{0,1:T(8,128)(2,1)}), bf16[16384,152]{0,1:T(8,128)(2,1)}) %all-gather.8.cloned.1.call-update) | async-done | bytes 4980752 | tf_op jit(solution)/shard_map/all_gather | solution.py:27
  423.1 8.7 %convolution_add_fusion = f32[16384,112]{0,1:T(8,128)} fusion(f32[16384,112]{0,1:T(8,128)} %fusion.5, bf16[16384,152]{0,1:T(8,128)(2,1)} %all-gather.8.cloned.1.call-done, bf16[112,152]{0,1:T(8,128)(2,1)S(1)} %copy-done.6), kind=kOutput, calls=%fused_computation | convolution fusion | flops 559677440 | bytes 19694848 | tf_op jit(solution)/shard_map/tf,df->td/dot_general | solution.py:29
  431.8 293.3 %all-reduce.3.cloned.1.call-done = (f32[16384,112]{0,1:T(8,128)}, f32[16384,112]{0,1:T(8,128)}) async-done(((f32[16384,112]{0,1:T(8,128)}, f32[16384,112]{0,1:T(8,128)}), (f32[16384,112]{0,1:T(8,128)}, f32[16384,112]{0,1:T(8,128)})) %all-reduce.3.cloned.1.call-update) | async-done | bytes 14680080 | tf_op jit(solution)/shard_map/psum | solution.py:19
  725.1 9.9 %add_convert_fusion = (bf16[16384,112]{0,1:T(8,128)(2,1)}, bf16[16384,112]{0,1:T(8,128)(2,1)S(1)}) fusion(f32[16384,112]{0,1:T(8,128)} %get-tuple-element.11, bf16[16384,112]{0,1:T(8,128)(2,1)} %bitcast.50, f32[16384,112]{0,1:T(8,128)} %get-tuple-element.10, bf16[16384,112]{0,1:T(8,128)(2,1)} %bitcast.46), kind=kLoop, calls=%fused_computation.1 | loop fusion | flops 11010048 | bytes 29360128 | tf_op jit(solution)/shard_map/convert_element_type | solution.py:30
  735.0 2.3 copy.29
  737.3 5.5 all-to-all-start.1
  742.8 4.4 copy.28
  747.1 38.6 %all-to-all-done.1 = bf16[8,2048,112]{1,2,0:T(8,128)(2,1)} async-done(((bf16[8,2048,112]{1,2,0:T(8,128)(2,1)}), bf16[8,2048,112]{1,2,0:T(8,128)(2,1)}, u32[]{:S(2)}, u32[]{:S(2)}) %all-to-all-start.1) | async-done | bytes 3670048 | tf_op jit(solution)/shard_map/all_to_all | solution.py:20
  785.8 5.5 all-to-all-start.3
  791.2 5.8 fusion.6
  797.0 4.9 convolution_bitcast_fusion.1
  801.9 2.2 convolution_bitcast_fusion
  804.1 6.0 copy.20
  810.1 24.1 %all-to-all-done.3 = bf16[8,2048,112]{1,2,0:T(8,128)(2,1)} async-done(((bf16[8,2048,112]{1,2,0:T(8,128)(2,1)}), bf16[8,2048,112]{1,2,0:T(8,128)(2,1)}, u32[]{:S(2)}, u32[]{:S(2)}) %all-to-all-start.3) | async-done | bytes 3670048 | tf_op jit(solution)/shard_map/all_to_all | solution.py:31
  834.2 6.1 copy.21
  (33 shorter events, 2.4 us)
Async XLA Ops:
  7.2 143.8 %copy-start = (bf16[112,152]{0,1:T(8,128)(2,1)S(1)}, bf16[112,152]{0,1:T(8,128)(2,1)}, u32[]{:S(2)}) copy-start(bf16[112,152]{0,1:T(8,128)(2,1)} %param.6) | copy-start | bytes 102148
  7.2 164.3 %reduce-scatter.8.cloned.1.call-start = ((), (), s32[]{:S(2)}) async-start(), calls=%async_computation.10 | async-start | bytes 11206656 | tf_op jit(solution)/shard_map/reduce_scatter | solution.py:23
  62.8 2.3 copy-start.5
  63.3 1.8 copy-start.4
  70.5 166.5 %reduce-scatter.6.cloned.1.call-start = ((), (), s32[]{:S(2)}) async-start(), calls=%async_computation.8 | async-start | bytes 11206656 | tf_op jit(solution)/shard_map/reduce_scatter | solution.py:13
  143.3 2.3 copy-start.6
  143.8 1.8 copy-start.2
  150.9 150.9 %reduce-scatter.4.cloned.1.call-start = ((), (), s32[]{:S(2)}) async-start(), calls=%async_computation.7 | async-start | bytes 11206656 | tf_op jit(solution)/shard_map/reduce_scatter | solution.py:12
  158.3 186.0 %all-gather.6.cloned.1.call-start = ((), (), s32[]{:S(2)}) async-start(), calls=%async_computation.11 | async-start | bytes 5603328 | tf_op jit(solution)/shard_map/all_gather | solution.py:26
  305.9 77.7 %all-gather.4.cloned.1.call-start = ((), (), s32[]{:S(2)}) async-start(), calls=%async_computation.9 | async-start | bytes 5603328 | tf_op jit(solution)/shard_map/all_gather | solution.py:17
  306.5 116.5 %all-gather.8.cloned.1.call-start = ((), (), s32[]{:S(2)}) async-start(), calls=%async_computation.12 | async-start | bytes 5603328 | tf_op jit(solution)/shard_map/all_gather | solution.py:27
  307.1 418.0 %all-reduce.3.cloned.1.call-start = ((), (), s32[]{:S(2)}) async-start(), calls=%async_computation.13 | async-start | bytes 29360128 | tf_op jit(solution)/shard_map/psum | solution.py:19
  737.3 48.5 %all-to-all-start.1 = ((bf16[8,2048,112]{1,2,0:T(8,128)(2,1)}), bf16[8,2048,112]{1,2,0:T(8,128)(2,1)}, u32[]{:S(2)}, u32[]{:S(2)}) async-start(bf16[8,2048,112]{1,2,0:T(8,128)(2,1)} %bitcast.57), calls=%async_computation.3 | async-start | bytes 7340032 | tf_op jit(solution)/shard_map/all_to_all | solution.py:20
  785.8 48.4 %all-to-all-start.3 = ((bf16[8,2048,112]{1,2,0:T(8,128)(2,1)}), bf16[8,2048,112]{1,2,0:T(8,128)(2,1)}, u32[]{:S(2)}, u32[]{:S(2)}) async-start(bf16[8,2048,112]{1,2,0:T(8,128)(2,1)} %bitcast.56), calls=%async_computation.6 | async-start | bytes 7340032 | tf_op jit(solution)/shard_map/all_to_all | solution.py:31
  791.2 5.8 copy-start.3
  791.2 10.6 %slice-start = ((s8[4980736]{0:T(1024)(128)(4,1)}), s8[4194304]{0:T(1024)(128)(4,1)S(1)}, s32[]{:S(2)}) async-start(s8[4980736]{0:T(1024)(128)(4,1)} %bitcast.52), calls=%async_computation.14 | async-start | bytes 8388608
  797.0 4.9 slice-start.1
  834.2 6.1 copy-start.1
Sparse Core Ops, SparseCore 0:
  70.6 100.7 reduce-scatter.7
  174.0 62.9 reduce-scatter.5
  239.5 62.2 reduce-scatter.3
  306.1 38.1 all-gather.5
  345.9 37.6 all-gather.3
  385.3 37.6 all-gather.7
  431.9 293.1 all-reduce.2
where the time goes:
time: 848 us; the launch traced here: 847 us
  waiting for transfers between devices  603 us (71%)
  blocking collectives  116 us (14%)
  matrix products  52.3 us (6%)
  local copies, waits for them, and re-layouts  35.6 us (4%)
  between operations  14.2 us (2%)
  other arithmetic  14 us (2%)
  starting transfers between devices  11.2 us (1%)
    psum x1, waiting for transfers between devices, device_pass(): lax.psum(out_part, 'tp')  293 us
    all_to_all x1, blocking collectives, device_pass(): x_cols = lax.all_to_all(x_rows, 'dp', 1, 0, tiled=True)  66.8 us
    reduce_scatter x1, waiting for transfers between devices, device_pass(): up_pre = lax.psum_scatter(up_part, 'dp', scatter_dimension=0, tiled=True)  65.5 us
    reduce_scatter x1, waiting for transfers between devices, device_pass(): lax.psum_scatter(gate_part, 'dp', scatter_dimension=0, tiled=True)  64.8 us
    all_to_all x1, blocking collectives, device_pass(): dy_cols = lax.all_to_all(dy_rows, 'dp', 1, 0, tiled=True)  49.6 us
    all_to_all x1, waiting for transfers between devices, device_pass(): y_rows = lax.all_to_all(y_cols, 'dp', 0, 1, tiled=True)  38.6 us
    all_gather x1, waiting for transfers between devices, device_pass(): gate_all = lax.all_gather(d_gate, 'dp', axis=0, tiled=True)  37.1 us
    all_gather x1, waiting for transfers between devices, device_pass(): up_all = lax.all_gather(d_up, 'dp', axis=0, tiled=True)  32.9 us
  transfers between devices with their start and end apart: 9, of which 9 were waited for; matrix products, arithmetic and copies ran while one was open for 7% of the time, Pallas kernels for 0%

commit v1 on v0

v1 whole, which is shorter than its diff:
```python
import jax
import jax.numpy as jnp
from jax import lax
from jax.sharding import PartitionSpec as P

NZ, NY = 8, 4


def solution(mesh):
    z_groups = [[z * NY + y for z in range(NZ)] for y in range(NY)]
    y_groups = [[z * NY + y for y in range(NY)] for z in range(NZ)]

    def grads(x, dy, wg, wu, wd):
        f32 = jnp.float32
        a = jnp.einsum('td,fd->tf', x, wg, preferred_element_type=f32)
        b = jnp.einsum('td,fd->tf', x, wu, preferred_element_type=f32)
        g = jnp.einsum('td,fd->tf', dy, wd, preferred_element_type=f32)
        s = jax.nn.sigmoid(a)
        silu = a * s
        h = (silu * b).astype(jnp.bfloat16)
        da = (g * b * s * (1.0 + a * (1.0 - s))).astype(jnp.bfloat16)
        db = (g * silu).astype(jnp.bfloat16)
        return h, da, db

    def device_pass(x, gate, up, down, dy):
        f32 = jnp.float32
        tp = lax.axis_index('tp')
        z = tp // NY
        w = jnp.concatenate([gate.T, up.T, down], axis=0)
        w_own = lax.all_gather(w, 'dp', axis=1, tiled=True)
        w_q = lax.all_gather(w_own, 'tp', axis=0, axis_index_groups=z_groups, tiled=False)
        wg = w_q[:, 0:152].reshape(NZ * 152, 896)
        wu = w_q[:, 152:304].reshape(NZ * 152, 896)
        wd = w_q[:, 304:456].reshape(NZ * 152, 896)
        xr = lax.dynamic_slice_in_dim(x, z * 256, 256, 0)
        dyr = lax.dynamic_slice_in_dim(dy, z * 256, 256, 0)
        h, da, db = grads(xr, dyr, wg, wu, wd)
        yp = jnp.dot(h, wd, preferred_element_type=f32)
        ys = lax.psum_scatter(yp, 'tp', scatter_dimension=0, axis_index_groups=y_groups, tiled=True)
        x64 = lax.dynamic_slice_in_dim(x, tp * 64, 64, 0)
        yr = (x64.astype(f32) + ys).astype(jnp.bfloat16)
        y_out = lax.all_gather(yr, 'tp', axis=0, tiled=True)
        dxp = jnp.dot(da, wg, preferred_element_type=f32) + jnp.dot(db, wu, preferred_element_type=f32)
        dxs = lax.psum_scatter(dxp, 'tp', scatter_dimension=0, axis_index_groups=y_groups, tiled=True)
        dy64 = lax.dynamic_slice_in_dim(dy, tp * 64, 64, 0)
        dxr = (dy64.astype(f32) + dxs).astype(jnp.bfloat16)
        dx_out = lax.all_gather(dxr, 'tp', axis=0, tiled=True)
        h2, da2, db2 = grads(x, dy, w_own[0:152], w_own[152:304], w_own[304:456])
        dg = jnp.einsum('td,tf->df', x, da2, preferred_element_type=f32)
        du = jnp.einsum('td,tf->df', x, db2, preferred_element_type=f32)
        dd = jnp.einsum('td,tf->df', dy, h2, preferred_element_type=f32)
        dall = jnp.concatenate([dg, du, dd], axis=1)
        dall = lax.psum_scatter(dall, 'dp', scatter_dimension=0, tiled=True)
        return y_out, dx_out, dall[:, 0:152], dall[:, 152:304], dall[:, 304:456].T

    row_spec = P('dp', None)
    weight_spec = P('dp', 'tp')
    down_spec = P('tp', 'dp')
    return jax.shard_map(device_pass, mesh=mesh,
                         in_specs=(row_spec, weight_spec, weight_spec, down_spec, row_spec),
                         out_specs=(row_spec, row_spec, weight_spec, weight_spec, down_spec),
                         check_vma=False)
```

time: 848 us -> 383 us (0.45)
  waiting for transfers between devices: 603 us -> 297 us
  blocking collectives: 116 us -> 16.6 us
  matrix products: 52.3 us -> 25.8 us
  local copies, waits for them, and re-layouts: 35.6 us -> 21.1 us
  starting transfers between devices: 11.2 us -> 0.43 us
  other arithmetic: 14 us -> 3.58 us
    psum x1 -> x0, waiting for transfers between devices: 293 us -> none  [device_pass(): lax.psum(out_part, 'tp')]
    all_gather x3, waiting for transfers between devices: 103 us -> 234 us  [the longest x1 80.3 us: device_pass(): dx_out = lax.all_gather(dxr, 'tp', axis=0, tiled=True)]
    reduce_scatter x3 -> x2, waiting for transfers between devices: 143 us -> 25.8 us  [the longest x1 25.8 us: device_pass(): lax.psum_scatter(dxp, 'tp', scatter_dimension=0, axis_index_groups=y_grou...]
    all_to_all x2 -> x0, blocking collectives: 116 us -> none  [the longest x1 66.8 us: device_pass(): x_cols = lax.all_to_all(x_rows, 'dp', 1, 0, tiled=True)]
    all_to_all x2 -> x0, waiting for transfers between devices: 62.7 us -> none  [the longest x1 38.6 us: device_pass(): y_rows = lax.all_to_all(y_cols, 'dp', 0, 1, tiled=True)]
    unnamed x7, waiting for transfers between devices: 1.14 us -> 37.1 us
    dot_general x9 -> x12, matrix products: 52.3 us -> 25.8 us  [the longest x2 6.96 us: grads(): a = jnp.einsum('td,fd->tf', x, wg, preferred_element_type=f32)]
    all_gather x0 -> x1, blocking collectives: none -> 16.6 us  [device_pass(): w_own = lax.all_gather(w, 'dp', axis=1, tiled=True)]
  transfers between devices with their start and end apart: 9 -> 6, of which waited for: 9 -> 5; matrix products, arithmetic and copies ran while one was open for 7% -> 7% of each run, Pallas kernels for 0% -> 0%
where the time goes in v1:
time: 383 us; the launch traced here: 379 us
  waiting for transfers between devices  297 us (78%)
  matrix products  25.8 us (7%)
  local copies, waits for them, and re-layouts  21.1 us (6%)
  blocking collectives  16.6 us (4%)
  between operations  14.4 us (4%)
    all_gather x1, waiting for transfers between devices, device_pass(): dx_out = lax.all_gather(dxr, 'tp', axis=0, tiled=True)  80.3 us
    all_gather x1, waiting for transfers between devices, device_pass(): y_out = lax.all_gather(yr, 'tp', axis=0, tiled=True)  77 us
    all_gather x1, waiting for transfers between devices, device_pass(): lax.all_gather(w_own, 'tp', axis=0, axis_index_groups=z_groups, tiled=False)  77 us
    unnamed x7, waiting for transfers between devices  37.1 us
    reduce_scatter x1, waiting for transfers between devices, device_pass(): lax.psum_scatter(dxp, 'tp', scatter_dimension=0, axis_index_groups=y_grou...  25.8 us
    all_gather x1, blocking collectives, device_pass(): w_own = lax.all_gather(w, 'dp', axis=1, tiled=True)  16.6 us
    unnamed x37, local copies, waits for them, and re-layouts  15.2 us
  transfers between devices with their start and end apart: 6, of which 5 were waited for; matrix products, arithmetic and copies ran while one was open for 7% of the time, Pallas kernels for 0%

profile of v1, /device:TPU:1, one launch (start us, length us, event | category | flops | bytes accessed | tf_op | source)
XLA Modules:
  0.0 379.2 jit_solution(329055930322899648)
XLA Ops:
  7.2 0.9 copy.13
  8.1 0.9 copy.14
  9.0 0.9 copy.15
  9.9 16.6 %all_gather.15 = bf16[456,896]{0,1:T(8,128)(2,1)S(1)} all-gather(bf16[456,112]{0,1:T(8,128)(2,1)S(1)} %pad_maximum_fusion.1), channel_id=1, replica_groups=mesh['tp'=32,'dp'=8] {'dp'}, dimensions={1}, use_global_device_ids=true | all-gather | bytes 919296 | tf_op jit(solution)/shard_map/all_gather | solution.py:30
  26.6 1.2 copy.16
  27.9 77.0 %all-gather.9.cloned.1.call-done = bf16[3648,896]{1,0:T(8,128)(2,1)} async-done(((bf16[456,896]{1,0:T(8,128)(2,1)}), bf16[3648,896]{1,0:T(8,128)(2,1)}) %all-gather.9.cloned.1.call-update) | async-done | bytes 6537232 | tf_op jit(solution)/shard_map/all_gather | solution.py:31
  104.9 3.5 fusion.26
  108.4 2.2 fusion.11
  110.6 2.2 fusion.9
  112.9 1.0 copy-done.12
  113.9 1.9 fusion.2
  115.9 4.7 %convolution_bitcast_fusion = f32[2048,152]{0,1:T(8,128)} fusion(bf16[2048,896]{1,0:T(8,128)(2,1)} %param.5, bf16[456,896]{0,1:T(8,128)(2,1)S(1)} %all_gather.15), kind=kOutput, calls=%fused_computation | convolution fusion | flops 557842432 | bytes 5373952 | tf_op jit(solution)/shard_map/td,fd->tf/dot_general | solution.py:15
  120.6 2.8 convolution_bitcast_fusion.1
  123.5 2.0 fusion.7
  125.5 1.0 fusion.3
  126.6 1.9 convolution_add_fusion
  128.8 4.0 %convolution_bitcast_fusion.2 = f32[2048,152]{0,1:T(8,128)S(1)} fusion(bf16[2048,896]{1,0:T(8,128)(2,1)} %param.9, bf16[456,896]{0,1:T(8,128)(2,1)S(1)} %all_gather.15), kind=kOutput, calls=%fused_computation.2 | convolution fusion | flops 557842432 | bytes 5373952 | tf_op jit(solution)/shard_map/td,fd->tf/dot_general | solution.py:17
  132.8 1.0 convolution_bitcast_fusion.4
  133.7 1.0 copy-done.6
  135.1 1.0 convolution_bitcast_fusion.3
  136.1 1.1 convolution_bitcast_fusion.5
  137.3 1.7 copy.17
  139.2 1.7 add_convert_fusion.1
  140.9 25.8 %reduce-scatter.8.cloned.1.call-done = f32[64,896]{1,0:T(8,128)} async-done(((f32[256,896]{1,0:T(8,128)}), f32[64,896]{1,0:T(8,128)}) %reduce-scatter.8.cloned.1.call-update) | async-done | bytes 229392 | tf_op jit(solution)/shard_map/reduce_scatter | solution.py:44
  166.7 1.7 add_convert_fusion
  168.4 37.0 %reduce-scatter.10.cloned.1.call-done = f32[112,456]{1,0:T(8,128)} async-done(((f32[896,456]{1,0:T(8,128)}), f32[112,456]{1,0:T(8,128)}) %reduce-scatter.10.cloned.1.call-update) | async-done | bytes 204304
  205.5 1.2 fusion.27
  206.6 0.7 copy.21
  208.8 77.0 %all-gather.5.cloned.1.call-done = bf16[2048,896]{1,0:T(8,128)(2,1)} async-done(((bf16[64,896]{1,0:T(8,128)(2,1)}), bf16[2048,896]{1,0:T(8,128)(2,1)}) %all-gather.5.cloned.1.call-update) | async-done | bytes 3670032 | tf_op jit(solution)/shard_map/all_gather | solution.py:42
  285.9 80.3 %all-gather.7.cloned.1.call-done = bf16[2048,896]{1,0:T(8,128)(2,1)} async-done(((bf16[64,896]{1,0:T(8,128)(2,1)}), bf16[2048,896]{1,0:T(8,128)(2,1)}) %all-gather.7.cloned.1.call-update) | async-done | bytes 3670032 | tf_op jit(solution)/shard_map/all_gather | solution.py:47
  366.2 4.3 %copy.24 = bf16[2048,896]{1,0:T(8,128)(2,1)} copy(bf16[2048,896]{1,0:T(8,128)(2,1)} %all-gather.5.cloned.1.call-done) | data formatting | bytes 7340032
  370.5 1.8 copy.25
  (43 shorter events, 2.7 us)
Async XLA Ops:
  7.2 97.7 %all-gather.9.cloned.1.call-start = ((), (), s32[]{:S(2)}) async-start(), calls=%async_computation.7 | async-start | bytes 7354368 | tf_op jit(solution)/shard_map/all_gather | solution.py:31
  27.8 111.3 %reduce-scatter.6.cloned.1.call-start = ((), (), s32[]{:S(2)}) async-start(), calls=%async_computation.3 | async-start | bytes 1146880 | tf_op jit(solution)/shard_map/reduce_scatter | solution.py:39
  108.3 2.2 copy-start.2
  108.4 4.5 %copy-start.4 = (bf16[8,152,896]{2,1,0:T(8,128)(2,1)}, bf16[8,152,896]{2,1,0:T(8,128)(2,1)S(1)}, u32[]{:S(2)}) copy-start(bf16[8,152,896]{2,1,0:T(8,128)(2,1)S(1)} %get-tuple-element.6) | copy-start | bytes 6537220
  110.6 2.3 copy-start.10
  112.8 1.1 copy-start.12
  115.8 50.9 %reduce-scatter.8.cloned.1.call-start = ((), (), s32[]{:S(2)}) async-start(), calls=%async_computation.5 | async-start | bytes 1146880 | tf_op jit(solution)/shard_map/reduce_scatter | solution.py:44
  115.9 4.8 %copy-start = (bf16[2048,896]{1,0:T(8,128)(2,1)S(1)}, bf16[2048,896]{1,0:T(8,128)(2,1)}, u32[]{:S(2)}) copy-start(bf16[2048,896]{1,0:T(8,128)(2,1)} %param.5) | copy-start | bytes 11010052
  120.6 2.8 copy-start.5
  120.6 4.9 %copy-start.13 = (f32[256,1216]{0,1:T(8,128)S(1)}, f32[256,1216]{0,1:T(8,128)}, u32[]{:S(2)}) copy-start(f32[256,1216]{0,1:T(8,128)} %copy-done.12) | copy-start | bytes 3735556
  123.5 2.0 copy-start.3
  123.5 2.1 copy-start.11
  128.5 4.2 %copy-start.8 = (f32[2048,152]{0,1:T(8,128)S(1)}, f32[2048,152]{0,1:T(8,128)}, u32[]{:S(2)}) copy-start(f32[2048,152]{0,1:T(8,128)} %convolution_bitcast_fusion) | copy-start | bytes 3735556
  128.5 76.9 %reduce-scatter.10.cloned.1.call-start = ((), (), s32[]{:S(2)}) async-start(), calls=%async_computation.8 | async-start | bytes 2064384
  128.7 4.0 %copy-start.1 = (bf16[2048,896]{1,0:T(8,128)(2,1)S(1)}, bf16[2048,896]{1,0:T(8,128)(2,1)}, u32[]{:S(2)}) copy-start(bf16[2048,896]{1,0:T(8,128)(2,1)} %param.5) | copy-start | bytes 11010052
  132.7 2.0 copy-start.6
  132.7 2.4 copy-start.9
  139.1 146.8 %all-gather.5.cloned.1.call-start = ((), (), s32[]{:S(2)}) async-start(), calls=%async_computation.4 | async-start | bytes 3784704 | tf_op jit(solution)/shard_map/all_gather | solution.py:42
  140.9 225.3 %all-gather.7.cloned.1.call-start = ((), (), s32[]{:S(2)}) async-start(), calls=%async_computation.6 | async-start | bytes 3784704 | tf_op jit(solution)/shard_map/all_gather | solution.py:47
  366.2 4.3 %copy-start.7 = (bf16[2048,896]{1,0:T(8,128)(2,1)S(1)}, bf16[2048,896]{1,0:T(8,128)(2,1)}, u32[]{:S(2)}) copy-start(bf16[2048,896]{1,0:T(8,128)(2,1)} %all-gather.7.cloned.1.call-done) | copy-start | bytes 11010052
Sparse Core Ops, SparseCore 0:
  28.0 76.8 all-gather.8
  115.9 22.3 reduce-scatter.5
  141.5 25.1 reduce-scatter.7
  169.7 35.7 reduce-scatter.9
  207.9 77.9 all-gather.4
  288.9 77.2 all-gather.6

commit v2 on v0

v2 whole, which is shorter than its diff:
```python
import functools

import jax
import jax.numpy as jnp
from jax import lax
from jax.experimental import pallas as pl
from jax.experimental.pallas import tpu as pltpu
from jax.sharding import PartitionSpec as P

MESH = pl.DeviceIdType.MESH
BF16, F32 = jnp.bfloat16, jnp.float32
NX, NY = 4, 4
LANES = 128


def pad_blocks(tiles, db):
    off = LANES - db
    lane = lax.broadcasted_iota(jnp.int32, tiles[0].shape, 1)
    blocks = []
    for d in range(8):
        s = off * d
        cur = pltpu.roll(tiles[d], s, 1) if (d < 7 and s) else (tiles[d] if d < 7 else None)
        prev = pltpu.roll(tiles[d - 1], s, 1) if d else None
        if cur is None:
            b = prev
        elif prev is None:
            b = cur
        else:
            b = jnp.where(lane < s, prev, cur)
        blocks.append(jnp.where(lane < db, b, 0.0))
    return blocks


def unpad_tiles(blocks, db):
    off = LANES - db
    lane = lax.broadcasted_iota(jnp.int32, blocks[0].shape, 1)
    tiles = []
    for q in range(7):
        s = off * q
        a = pltpu.roll(blocks[q], (LANES - s) % LANES, 1) if s else blocks[q]
        b = pltpu.roll(blocks[q + 1], db - s, 1) if (db - s) % LANES else blocks[q + 1]
        tiles.append(jnp.where(lane < db - s, a, b))
    return tiles


def col_block(d):
    return (d % 2) * NX + d // 2


def nt(a, b):
    return lax.dot_general(a, b, (((1,), (1,)), ((), ())), preferred_element_type=F32)


def nn(a, b):
    return lax.dot_general(a, b, (((1,), (0,)), ((), ())), preferred_element_type=F32)


def mlp_kernel(cfg, w_ref, x_hbm, dy_hbm, y_hbm, dx_hbm, dw_ref,
               xv, dyv, xp, dyp, W, yacc, dxacc, ysend, dxsend, yrs, dxrs, yv, dxv,
               wown, dwacc, dwp, dwr1, dwr2,
               in_sem, out_sem, s_gu, s_d, s_rs, s_y, s_dx, s_dw,
               r_gz, r_gx, r_gp, r_dx4, r_dz, r_dp, r_ys, r_dxs, r_yz, r_yy, r_xy, r_xz, r_w1, r_w2):
    NZ, FP, DB = cfg["NZ"], cfg["FP"], cfg["DB"]
    T, D = xv.shape
    RZ = T // NZ
    R1 = RZ // NY
    H = NZ // 2
    KP = 8 * LANES

    t = lax.axis_index("tp")
    d = lax.axis_index("dp")
    z, y = lax.div(t, NY), lax.rem(t, NY)
    x, c = lax.div(d, 2), lax.rem(d, 2)

    def wrap(v, n):
        return lax.rem(v + n, n)

    def dev(dz=0, dy_=0, dx_=0, core=None):
        tp = wrap(z + dz, NZ) * NY + wrap(y + dy_, NY)
        dp = wrap(x + dx_, NX) * 2 + (c if core is None else core)
        return {"tp": tp, "dp": dp}

    partner = dev(core=1 - c)

    def mo(v, m):
        return pl.multiple_of(v, m)

    def remote(src, dst, ssem, rsem, to):
        return pltpu.make_async_remote_copy(src_ref=src, dst_ref=dst, send_sem=ssem, recv_sem=rsem,
                                            device_id=to, device_id_type=MESH)

    def arrived(dst, rsem):
        remote(dst, dst, s_gu.at[0], rsem, partner).wait_recv()

    def zs_of(m):
        if m == 0:
            return z
        k = (m + 1) // 2
        return wrap(z - k, NZ) if m % 2 else wrap(z + k, NZ)

    def rows_w(zs):
        return pl.ds(mo(zs * FP, FP), FP)

    def half_w(cc):
        return pl.ds(mo(cc * (NX * LANES), NX * LANES), NX * LANES)

    def blk_w(xs, cc):
        return pl.ds(mo((cc * NX + xs) * LANES, LANES), LANES)

    def gu(zs, xs):
        return W.at[0:2, rows_w(zs), blk_w(xs, c)]

    def gu_half(zs, xs, h):
        return W.at[h, rows_w(zs), blk_w(xs, c)]

    def gu_all(zs, cc):
        return W.at[0:2, rows_w(zs), half_w(cc)]

    def dn(zs, xs):
        return W.at[2, rows_w(zs), blk_w(xs, c)]

    def dn_all(zs, cc):
        return W.at[2, rows_w(zs), half_w(cc)]

    def dn_half(zs, h):
        w2 = NX * LANES // 2
        return W.at[2, rows_w(zs), pl.ds(mo(c * (NX * LANES) + h * w2, w2), w2)]

    def rows(buf, zs, ys):
        return buf.at[pl.ds(mo((zs * NY + ys) * R1, R1), R1)]

    def rows_half(buf, zs, ys, h):
        return buf.at[pl.ds(mo((zs * NY + ys) * R1 + h * (R1 // 2), R1 // 2), R1 // 2)]

    def rows_z(buf, zs):
        return buf.at[pl.ds(mo(zs * RZ, RZ), RZ)]

    barrier = pltpu.get_barrier_semaphore()
    peers = [dev(dz=1), dev(dz=-1), dev(dy_=1), dev(dy_=-1), dev(dy_=2), dev(dx_=1), dev(dx_=-1), dev(dx_=2), partner]
    for p in peers:
        pl.semaphore_signal(barrier, inc=1, device_id=p, device_id_type=MESH)

    ld_x = pltpu.make_async_copy(x_hbm, xv, in_sem.at[0])
    ld_dy = pltpu.make_async_copy(dy_hbm, dyv, in_sem.at[1])
    ld_x.start()
    ld_dy.start()
    W[:, rows_w(z), blk_w(x, c)] = w_ref[...]
    pl.semaphore_wait(barrier, len(peers))

    def send_d_own():
        for i, dx_ in enumerate((1, -1, 2)):
            remote(w_ref.at[2], dn(z, x), s_d.at[0], r_dx4.at[i], dev(dx_=dx_)).start()

    def wait_d_own():
        for i, dx_ in enumerate((-1, 1, 2)):
            arrived(dn(z, wrap(x + dx_, NX)), r_dx4.at[i])

    def send_d_z(k):
        zm, zp = wrap(z - k, NZ), wrap(z + k, NZ)
        if k < H - 1:
            remote(dn_all(zm, c), dn_all(zm, c), s_d.at[1], r_dz.at[0, k], dev(dz=1)).start()
            remote(dn_all(zp, c), dn_all(zp, c), s_d.at[1], r_dz.at[1, k], dev(dz=-1)).start()
        elif k == H - 1:
            remote(dn_half(zm, 0), dn_half(zm, 0), s_d.at[1], r_dz.at[0, k], dev(dz=1)).start()
            remote(dn_half(zp, 1), dn_half(zp, 1), s_d.at[1], r_dz.at[1, k], dev(dz=-1)).start()

    def wait_d_z(k):
        zm, zp = wrap(z - k, NZ), wrap(z + k, NZ)
        if k < H:
            arrived(dn_all(zm, c), r_dz.at[0, k - 1])
            arrived(dn_all(zp, c), r_dz.at[1, k - 1])
        else:
            arrived(dn_half(zm, 0), r_dz.at[0, k - 1])
            arrived(dn_half(zp, 1), r_dz.at[1, k - 1])

    def send_d_p(m):
        zs = zs_of(m)
        remote(dn_all(zs, c), dn_all(zs, c), s_d.at[2], r_dp.at[m], partner).start()

    def send_g_z(k):
        zm, zp = wrap(z - k, NZ), wrap(z + k, NZ)
        if k < H - 1:
            sm = w_ref.at[0:2] if k == 0 else gu(zm, x)
            sp = w_ref.at[0:2] if k == 0 else gu(zp, x)
            remote(sm, gu(zm, x), s_gu.at[0], r_gz.at[0, k], dev(dz=1)).start()
            remote(sp, gu(zp, x), s_gu.at[0], r_gz.at[1, k], dev(dz=-1)).start()
        elif k == H - 1:
            remote(gu_half(zm, x, 0), gu_half(zm, x, 0), s_gu.at[0], r_gz.at[0, k], dev(dz=1)).start()
            remote(gu_half(zp, x, 1), gu_half(zp, x, 1), s_gu.at[0], r_gz.at[1, k], dev(dz=-1)).start()

    def wait_g_z(k):
        zm, zp = wrap(z - k, NZ), wrap(z + k, NZ)
        if k < H:
            arrived(gu(zm, x), r_gz.at[0, k - 1])
            arrived(gu(zp, x), r_gz.at[1, k - 1])
        else:
            arrived(gu_half(zm, x, 0), r_gz.at[0, k - 1])
            arrived(gu_half(zp, x, 1), r_gz.at[1, k - 1])

    def send_g_x(m):
        zs = zs_of(m)
        src = w_ref.at[0:2] if m == 0 else gu(zs, x)
        remote(src, gu(zs, x), s_gu.at[1], r_gx.at[0, m], dev(dx_=1)).start()
        remote(src, gu(zs, x), s_gu.at[1], r_gx.at[1, m], dev(dx_=-1)).start()

    def fwd_g_x(m):
        zs = zs_of(m)
        xm, xq = wrap(x - 1, NX), wrap(x + 1, NX)
        arrived(gu(zs, xm), r_gx.at[0, m])
        if m % 2 == 0:
            remote(gu(zs, xm), gu(zs, xm), s_gu.at[1], r_gx.at[2, m], dev(dx_=1)).start()
        arrived(gu(zs, xq), r_gx.at[1, m])
        if m % 2 == 1:
            remote(gu(zs, xq), gu(zs, xq), s_gu.at[1], r_gx.at[2, m], dev(dx_=-1)).start()

    def send_g_p(m):
        zs = zs_of(m)
        arrived(gu(zs, wrap(x + 2, NX)), r_gx.at[2, m])
        remote(gu_all(zs, c), gu_all(zs, c), s_gu.at[2], r_gp.at[m], partner).start()

    def wait_p(m):
        zs = zs_of(m)
        arrived(gu_all(zs, 1 - c), r_gp.at[m])
        arrived(dn_all(zs, 1 - c), r_dp.at[m])

    def pad_rows(src, dst):
        def body(i, _):
            r = pl.ds(mo(i * 32, 32), 32)
            rs = pl.ds(mo(z * RZ + i * 32, 32), 32)
            v = src[rs, :].astype(F32)
            blocks = pad_blocks([v[:, q * LANES:(q + 1) * LANES] for q in range(7)], DB)
            for dd in range(8):
                j = col_block(dd)
                dst[r, j * LANES:(j + 1) * LANES] = blocks[dd].astype(BF16)
            return 0
        lax.fori_loop(0, RZ // 32, body, 0)

    def act(a, b, g):
        s = jax.nn.sigmoid(a)
        silu = a * s
        h = (silu * b).astype(BF16)
        da = (g * b * s * (1.0 + a * (1.0 - s))).astype(BF16)
        db = (g * silu).astype(BF16)
        return h, da, db

    def slice_acts(m):
        r = rows_w(zs_of(m))
        a = nt(xp[...], W[0, r, :])
        b = nt(xp[...], W[1, r, :])
        g = nt(dyp[...], W[2, r, :])
        return act(a, b, g)

    def slice_y(m, h):
        r = rows_w(zs_of(m))
        p = nn(h, W[2, r, :])
        yacc[...] = p if m == 0 else yacc[...] + p

    def slice_dx(m, da, db):
        r = rows_w(zs_of(m))
        p = nn(da, W[0, r, :]) + nn(db, W[1, r, :])
        dxacc[...] = p if m == 0 else dxacc[...] + p

    def compute(m):
        h, da, db = slice_acts(m)
        slice_y(m, h)
        slice_dx(m, da, db)

    def unpad_rows(src, dst):
        def body(i, _):
            r = pl.ds(mo(i * 32, 32), 32)
            blocks = [src[r, col_block(dd) * LANES:(col_block(dd) + 1) * LANES] for dd in range(8)]
            for q, tile in enumerate(unpad_tiles(blocks, DB)):
                dst[r, q * LANES:(q + 1) * LANES] = tile
            return 0
        lax.fori_loop(0, RZ // 32, body, 0)

    def part(buf, ys):
        return buf.at[pl.ds(mo(ys * R1, R1), R1)]

    def send_rs(buf, rbuf, ssem, rsem):
        for i, dy_ in enumerate((1, -1, 2)):
            remote(part(buf, wrap(y + dy_, NY)), rbuf.at[i], ssem, rsem.at[i], dev(dy_=dy_)).start()

    def finish_rs(buf, rbuf, rsem, base, out):
        for i in range(3):
            arrived(rbuf.at[i], rsem.at[i])
        own = pl.ds(mo(y * R1, R1), R1)
        g = pl.ds(mo(t * R1, R1), R1)
        s = buf[own, :] + rbuf[0] + rbuf[1] + rbuf[2]
        out[g, :] = (base[g, :].astype(F32) + s).astype(BF16)

    def send_y_z(k):
        zm, zp = wrap(z - k, NZ), wrap(z + k, NZ)
        if k < H - 1:
            remote(rows(yv, zm, y), rows(yv, zm, y), s_y.at[0], r_yz.at[0, k], dev(dz=1)).start()
            remote(rows(yv, zp, y), rows(yv, zp, y), s_y.at[0], r_yz.at[1, k], dev(dz=-1)).start()
        elif k == H - 1:
            remote(rows_half(yv, zm, y, 0), rows_half(yv, zm, y, 0), s_y.at[0], r_yz.at[0, k], dev(dz=1)).start()
            remote(rows_half(yv, zp, y, 1), rows_half(yv, zp, y, 1), s_y.at[0], r_yz.at[1, k], dev(dz=-1)).start()

    def wait_y_z(k):
        zm, zp = wrap(z - k, NZ), wrap(z + k, NZ)
        if k < H:
            arrived(rows(yv, zm, y), r_yz.at[0, k - 1])
            arrived(rows(yv, zp, y), r_yz.at[1, k - 1])
        else:
            arrived(rows_half(yv, zm, y, 0), r_yz.at[0, k - 1])
            arrived(rows_half(yv, zp, y, 1), r_yz.at[1, k - 1])

    def send_y_y(m):
        b = rows(yv, zs_of(m), y)
        remote(b, b, s_y.at[1], r_yy.at[0, m], dev(dy_=1)).start()
        remote(b, b, s_y.at[1], r_yy.at[1, m], dev(dy_=-1)).start()

    def fwd_y_y(m):
        zs = zs_of(m)
        bm, bq = rows(yv, zs, wrap(y - 1, NY)), rows(yv, zs, wrap(y + 1, NY))
        arrived(bm, r_yy.at[0, m])
        if m % 2 == 0:
            remote(bm, bm, s_y.at[1], r_yy.at[2, m], dev(dy_=1)).start()
        arrived(bq, r_yy.at[1, m])
        if m % 2 == 1:
            remote(bq, bq, s_y.at[1], r_yy.at[2, m], dev(dy_=-1)).start()

    def end_y_y(m):
        zs = zs_of(m)
        arrived(rows(yv, zs, wrap(y + 2, NY)), r_yy.at[2, m])
        pltpu.make_async_copy(rows_z(yv, zs), rows_z(y_hbm, zs), out_sem.at[0, m]).start()

    SUB = (0, -1, 1, 2)

    def send_x_y():
        b = rows(dxv, z, y)
        for i, dy_ in enumerate((1, -1, 2)):
            remote(b, b, s_dx.at[0], r_xy.at[i], dev(dy_=dy_)).start()

    def wait_x_y(i):
        dy_ = (-1, 1, 2)[i]
        arrived(rows(dxv, z, wrap(y + dy_, NY)), r_xy.at[i])

    def send_x_z(k, s):
        zm, zp = wrap(z - k, NZ), wrap(z + k, NZ)
        ys = wrap(y + SUB[s], NY)
        if k < H - 1 or (k == H - 1 and s % 2 == 0):
            remote(rows(dxv, zm, ys), rows(dxv, zm, ys), s_dx.at[1], r_xz.at[0, k, s], dev(dz=1)).start()
        if k < H - 1 or (k == H - 1 and s % 2 == 1):
            remote(rows(dxv, zp, ys), rows(dxv, zp, ys), s_dx.at[1], r_xz.at[1, k, s], dev(dz=-1)).start()

    def wait_x_z(k, s):
        zm, zp = wrap(z - k, NZ), wrap(z + k, NZ)
        ys = wrap(y + SUB[s], NY)
        if k < H or s % 2 == 0:
            arrived(rows(dxv, zm, ys), r_xz.at[0, k - 1, s])
        if k < H or s % 2 == 1:
            arrived(rows(dxv, zp, ys), r_xz.at[1, k - 1, s])

    def out_x(m):
        zs = zs_of(m)
        pltpu.make_async_copy(rows_z(dxv, zs), rows_z(dx_hbm, zs), out_sem.at[1, m]).start()

    CH = cfg["CH"]
    n_chunks = T // CH

    def own_weights():
        def body(i, _):
            kind, r0 = lax.div(i, FP // 32), lax.rem(i, FP // 32)
            r = pl.ds(mo(z * FP + r0 * 32, 32), 32)
            v = W[kind, r, :].astype(F32)
            blocks = [v[:, col_block(dd) * LANES:(col_block(dd) + 1) * LANES] for dd in range(8)]
            o = pl.ds(mo(i * 32, 32), 32)
            for q, tile in enumerate(unpad_tiles(blocks, DB)):
                wown[o, q * LANES:(q + 1) * LANES] = tile.astype(BF16)
            return 0
        lax.fori_loop(0, 3 * FP // 32, body, 0)

    def dw_chunk(i):
        r = pl.ds(i * CH, CH)
        xb, dyb = xv[r, :], dyv[r, :]
        ab = nt(wown[0:2 * FP, :], xb)
        g = nt(wown[2 * FP:3 * FP, :], dyb)
        h, da, db = act(ab[0:FP], ab[FP:2 * FP], g)
        for q, (lhs, rhs) in enumerate(((da, xb), (db, xb), (h, dyb))):
            o = pl.ds(q * FP, FP)
            p = nn(lhs, rhs)
            dwacc[o, :] = p if i == 0 else dwacc[o, :] + p

    def dw_blocks():
        def body(i, _):
            r = pl.ds(mo(i * 32, 32), 32)
            v = dwacc[r, :]
            blocks = pad_blocks([v[:, q * LANES:(q + 1) * LANES] for q in range(7)], DB)
            for dd in range(8):
                dwp[col_block(dd), r, :] = blocks[dd]
            return 0
        lax.fori_loop(0, 3 * FP // 32, body, 0)

    def send_w1():
        src = dwp.at[pl.ds((1 - c) * NX, NX)]
        remote(src, dwr1, s_dw.at[0], r_w1.at[0], partner).start()

    def send_w2():
        arrived(dwr1, r_w1.at[0])
        for dx_ in (1, -1, 2, 0):
            xs = wrap(x + dx_, NX)
            dwp[c * NX + xs] = dwp[c * NX + xs] + dwr1[xs]
        for i, dx_ in enumerate((1, -1, 2)):
            xs = wrap(x + dx_, NX)
            remote(dwp.at[c * NX + xs], dwr2.at[i], s_dw.at[1], r_w2.at[i], dev(dx_=dx_)).start()

    def finish_w():
        for i in range(3):
            arrived(dwr2.at[i], r_w2.at[i])
        dw_ref[...] = dwp[c * NX + x] + dwr2[0] + dwr2[1] + dwr2[2]

    def ms(k):
        if k == 0:
            return (0,)
        return (2 * k - 1, 2 * k) if k < H else (NZ - 1,)

    send_g_z(0)
    send_d_own()
    send_g_x(0)
    ld_x.wait()
    pad_rows(xv, xp)
    wait_d_own()
    send_d_z(0)
    send_d_p(0)
    ld_dy.wait()
    pad_rows(dyv, dyp)

    last = NZ - 1
    acts = None
    for k in range(1, H + 3):
        if k <= H:
            wait_g_z(k)
            send_g_z(k)
            for m in ms(k):
                send_g_x(m)
        if k - 1 <= H:
            for m in ms(k - 1):
                fwd_g_x(m)
            if k >= 2:
                wait_d_z(k - 1)
                send_d_z(k - 1)
                for m in ms(k - 1):
                    send_d_p(m)
            for m in ms(k - 1):
                send_g_p(m)
        if k - 2 >= 0 and k - 2 < H:
            for m in ms(k - 2):
                wait_p(m)
                compute(m)
    wait_p(last)
    h, da, db = slice_acts(last)
    slice_y(last, h)
    unpad_rows(yacc, ysend)
    send_rs(ysend, yrs, s_rs.at[0], r_ys)
    slice_dx(last, da, db)
    unpad_rows(dxacc, dxsend)
    send_rs(dxsend, dxrs, s_rs.at[1], r_dxs)
    own_weights()
    finish_rs(ysend, yrs, r_ys, xv, yv)
    send_y_z(0)
    send_y_y(0)
    dw_chunk(0)
    wait_y_z(1)
    send_y_z(1)
    finish_rs(dxsend, dxrs, r_dxs, dyv, dxv)
    send_x_z(0, 0)
    send_x_y()
    for m in ms(1):
        send_y_y(m)
    nxt = 1

    def more():
        nonlocal nxt
        if nxt < n_chunks:
            dw_chunk(nxt)
            nxt += 1
            if nxt == n_chunks:
                dw_blocks()
                send_w1()

    for k in range(2, H + 1):
        more()
        wait_y_z(k)
        send_y_z(k)
        if k == 2:
            for i in range(3):
                wait_x_y(i)
                send_x_z(0, i + 1)
        for m in ms(k):
            send_y_y(m)
        for m in ms(k - 2):
            fwd_y_y(m)
        more()
        for s in range(4):
            wait_x_z(k - 1, s)
            send_x_z(k - 1, s)
        out_x(0) if k == 2 else [out_x(m) for m in ms(k - 2)]
    while nxt < n_chunks:
        more()
    for m in ms(H - 1):
        fwd_y_y(m)
    for m in ms(H):
        fwd_y_y(m)
    send_w2()
    for m in ms(H - 1):
        out_x(m)
    for m in range(NZ):
        end_y_y(m)
    for s in range(4):
        wait_x_z(H, s)
    out_x(last)
    finish_w()

    def sent(total, sem):
        remote(total, total, sem, r_w1.at[0], partner).wait_send()

    n1 = NZ - 1
    sent(W.at[0:2, 0:n1 * FP, 0:LANES], s_gu.at[0])
    sent(W.at[0:2, :, 0:3 * LANES], s_gu.at[1])
    sent(W.at[0:2, :, 0:NX * LANES], s_gu.at[2])
    sent(W.at[2, 0:FP, 0:3 * LANES], s_d.at[0])
    sent(W.at[2, 0:n1 * FP, 0:NX * LANES], s_d.at[1])
    sent(W.at[2, :, 0:NX * LANES], s_d.at[2])
    sent(yrs, s_rs.at[0])
    sent(dxrs, s_rs.at[1])
    sent(yv.at[0:n1 * R1], s_y.at[0])
    sent(yv.at[0:3 * NZ * R1], s_y.at[1])
    sent(dxv.at[0:3 * R1], s_dx.at[0])
    sent(dxv.at[0:4 * n1 * R1], s_dx.at[1])
    sent(dwr1, s_dw.at[0])
    sent(dwr2, s_dw.at[1])
    for m in range(NZ):
        zs = zs_of(m)
        pltpu.make_async_copy(rows_z(yv, zs), rows_z(y_hbm, zs), out_sem.at[0, m]).wait()
        pltpu.make_async_copy(rows_z(dxv, zs), rows_z(dx_hbm, zs), out_sem.at[1, m]).wait()


def mlp_call(cfg, w, x, dy):
    NZ, FP = cfg["NZ"], cfg["FP"]
    T, D = x.shape
    RZ = T // NZ
    R1 = RZ // NY
    H = NZ // 2
    KP = 8 * LANES
    dma = pltpu.SemaphoreType.DMA
    vm = pltpu.VMEM
    return pl.pallas_call(
        functools.partial(mlp_kernel, cfg),
        name="mlp",
        out_shape=(jax.ShapeDtypeStruct((T, D), BF16), jax.ShapeDtypeStruct((T, D), BF16),
                   jax.ShapeDtypeStruct((3 * FP, LANES), F32)),
        in_specs=[pl.BlockSpec(memory_space=pltpu.VMEM), pl.BlockSpec(memory_space=pl.ANY), pl.BlockSpec(memory_space=pl.ANY)],
        out_specs=(pl.BlockSpec(memory_space=pl.ANY), pl.BlockSpec(memory_space=pl.ANY), pl.BlockSpec(memory_space=pltpu.VMEM)),
        scratch_shapes=[
            vm((T, D), BF16), vm((T, D), BF16), vm((RZ, KP), BF16), vm((RZ, KP), BF16), vm((3, NZ * FP, KP), BF16),
            vm((RZ, KP), F32), vm((RZ, KP), F32), vm((RZ, D), F32), vm((RZ, D), F32),
            vm((3, R1, D), F32), vm((3, R1, D), F32), vm((T, D), BF16), vm((T, D), BF16),
            vm((3 * FP, D), BF16), vm((3 * FP, D), F32), vm((8, 3 * FP, LANES), F32),
            vm((NX, 3 * FP, LANES), F32), vm((3, 3 * FP, LANES), F32),
            dma((2,)), dma((2, NZ)), dma((3,)), dma((3,)), dma((2,)), dma((2,)), dma((2,)), dma((2,)),
            dma((2, H)), dma((3, NZ)), dma((NZ,)), dma((3,)), dma((2, H)), dma((NZ,)), dma((3,)), dma((3,)),
            dma((2, H)), dma((3, NZ)), dma((3,)), dma((2, H, 4)), dma((1,)), dma((3,)),
        ],
        compiler_params=pltpu.CompilerParams(collective_id=0, has_side_effects=True, vmem_limit_bytes=60 * 1024 * 1024),
    )(w, x, dy)


def solution(mesh):
    nz = mesh.shape["tp"] // NY

    def device_pass(x, gate, up, down, dy):
        db, f = gate.shape
        fp = -(-f // 32) * 32
        cfg = {"NZ": nz, "FP": fp, "DB": db, "CH": min(256, x.shape[0])}
        pad = lambda a: jnp.pad(a, ((0, fp - f), (0, LANES - db)))
        w = jnp.stack([pad(gate.T), pad(up.T), pad(down)])
        y, dx, dw = mlp_call(cfg, w, x, dy)
        dw = dw.reshape(3, fp, LANES)[:, :f, :db]
        return y, dx, dw[0].T, dw[1].T, dw[2]

    row, col, low = P("dp", None), P("dp", "tp"), P("tp", "dp")
    return jax.shard_map(device_pass, mesh=mesh, in_specs=(row, col, col, low, row),
                         out_specs=(row, row, col, col, low), check_vma=False)
```

time: 848 us -> 142 us (0.17)
  waiting for transfers between devices: 603 us -> 0 us
  Pallas kernels: 0 us -> 131 us
  blocking collectives: 116 us -> 0 us
  matrix products: 52.3 us -> 0 us
  local copies, waits for them, and re-layouts: 35.6 us -> 9.41 us
  between operations: 14.2 us -> 0.65 us
  other arithmetic: 14 us -> 0.66 us
  starting transfers between devices: 11.2 us -> 0 us
    psum x1 -> x0, waiting for transfers between devices: 293 us -> none  [device_pass(): lax.psum(out_part, 'tp')]
    reduce_scatter x3 -> x0, waiting for transfers between devices: 143 us -> none  [the longest x1 65.5 us: device_pass(): up_pre = lax.psum_scatter(up_part, 'dp', scatter_dimension=0, tiled=True)]
    pallas_call x0 -> x1, Pallas kernels: none -> 131 us  [mlp_call(): pl.pallas_call(functools.partial(mlp_kernel, cfg), name='mlp', out_shape=...]
    all_to_all x2 -> x0, blocking collectives: 116 us -> none  [the longest x1 66.8 us: device_pass(): x_cols = lax.all_to_all(x_rows, 'dp', 1, 0, tiled=True)]
    all_gather x3 -> x0, waiting for transfers between devices: 103 us -> none  [the longest x1 37.1 us: device_pass(): gate_all = lax.all_gather(d_gate, 'dp', axis=0, tiled=True)]
    all_to_all x2 -> x0, waiting for transfers between devices: 62.7 us -> none  [the longest x1 38.6 us: device_pass(): y_rows = lax.all_to_all(y_cols, 'dp', 0, 1, tiled=True)]
    dot_general x9 -> x0, matrix products: 52.3 us -> none  [the longest x1 8.7 us: device_pass(): jnp.einsum('tf,df->td', up_all, up_blk, preferred_element_type=jnp.float32)]
    unnamed x22 -> x4, local copies, waits for them, and re-layouts: 27.9 us -> 6.16 us
  transfers between devices with their start and end apart: 9 -> 0, of which waited for: 9 -> 0; matrix products, arithmetic and copies ran while one was open for 7% -> 0% of each run, Pallas kernels for 0% -> 0%
where the time goes in v2:
time: 142 us
  Pallas kernels  131 us (92%)
  local copies, waits for them, and re-layouts  9.41 us (7%)
    pallas_call x1, Pallas kernels, mlp_call(): pl.pallas_call(functools.partial(mlp_kernel, cfg), name='mlp', out_shape=...  131 us
    unnamed x4, local copies, waits for them, and re-layouts  6.16 us

profile of v2, /device:TPU:1, one launch (start us, length us, event | category | flops | bytes accessed | tf_op | source)
XLA Modules:
  0.0 141.6 jit_solution(1967374526967240317)
XLA Ops:
  0.6 0.8 pad_bitcast_fusion
  1.4 0.8 pad_bitcast_fusion.2
  2.2 0.7 pad_maximum_fusion.w_ref
  2.9 130.8 %mlp.1 = (bf16[2048,896]{1,0:T(8,128)(2,1)}, bf16[2048,896]{1,0:T(8,128)(2,1)}, f32[480,128]{1,0:T(8,128)}) custom-call(bf16[3,160,128]{2,1,0:T(8,128)(2,1)} %pad_maximum_fusion.w_ref, bf16[2048,896]{1,0:T(8,128)(2,1)} %x_hbm.1, bf16[2048,896]{1,0:T(8,128)(2,1)} %dy_hbm.1), custom_call_target="tpu_custom_call" | custom-call | tf_op jit(solution)/shard_map/mlp/pallas_call | solution.py:550
  133.8 1.7 %slice_bitcast_fusion = (f32[152,112]{1,0:T(8,128)}, f32[112,152]{0,1:T(8,128)}, f32[112,152]{0,1:T(8,128)}) fusion(f32[3,160,128]{2,1,0:T(8,128)} %bitcast.19), kind=kLoop, calls=%fused_computation.1 | loop fusion | bytes 408576 | tf_op jit(solution)/shard_map/squeeze | solution.py:582
  135.4 0.0 copy-start
  135.4 4.3 %copy.12 = bf16[2048,896]{1,0:T(8,128)(2,1)} copy(bf16[2048,896]{1,0:T(8,128)(2,1)} %get-tuple-element.21) | data formatting | bytes 7340032
  139.7 0.0 copy-done
  139.7 1.8 %copy.13 = bf16[2048,896]{1,0:T(8,128)(2,1)} copy(bf16[2048,896]{1,0:T(8,128)(2,1)S(1)} %copy-done) | data formatting | bytes 7340032
Async XLA Ops:
  135.4 4.3 %copy-start = (bf16[2048,896]{1,0:T(8,128)(2,1)S(1)}, bf16[2048,896]{1,0:T(8,128)(2,1)}, u32[]{:S(2)}) copy-start(bf16[2048,896]{1,0:T(8,128)(2,1)} %get-tuple-element.22) | copy-start | bytes 11010052
